TPU v7x, 32 devices: a whole 2x2x4 slice. The times are simulated.
32 devices in a mesh: space: 16 (over z, y, core), tm: 2 (over x).
Axes of the slice: x: 2, y: 2, z: 4, core: 2. Of those that a mesh axis runs over, the one named last changes fastest.
Arguments:
- row_orbitals: bfloat16 [8192, 2048], P('space', 'tm'), may hold values from -0.890625 to 0.890625
- column_orbitals: bfloat16 [256, 2048], P('space', 'tm'), may hold values from -0.890625 to 0.890625
- occupation: int32 [2048], replicated, may hold values from 0 to 2
- order: int32 [2048], replicated, may hold values from 0 to 2047, each once
- levels: float32 [2048], replicated, may hold values from 0.1 to 1
- times: float32 [2], replicated, may hold values from 0.05 to 1.5
- quad_weights: float32 [2], replicated, may hold values from 0.5 to 1.5
- freqs: float32 [8], replicated, may hold values from 0.1 to 4
Outputs:
- spectrum: float32 [8, 8192, 256], P(None, ('space', 'tm'))
Inputs may be any that keep to these rules, and one draw needn't show every extreme that they name: `order`: each index of 0 to 2047 once.
All inputs are finite; a program needn't handle non-finite values.
Results may differ from a plain program's by a relative error of at most 0.0026.
Values may be sent and summed in bfloat16 or wider, within the bound.
No kernel may reach another device: no remote copies, remote signals or barrier semaphores. Data moves between devices by JAX's collectives and lax.ppermute only.
A program may use at most 64 MiB of HBM per device.

v0:
```python
import jax
import jax.numpy as jnp
from jax import lax
from jax.sharding import PartitionSpec as P


def body(row_orbitals, column_orbitals, occupation, order, levels, times, quad_weights, freqs):
    energy = jnp.take(levels, order)
    filled = occupation.astype(jnp.float32) * 0.5
    rows_full = lax.all_to_all(row_orbitals, "tm", split_axis=0, concat_axis=1, tiled=True)
    decays = jnp.exp(-times[:, None] * energy[None, :])
    full_weight = filled[None, :] * decays
    empty_weight = (1.0 - filled)[None, :] * decays
    row_values = rows_full.astype(jnp.float32)[None]
    scaled_full = (row_values * full_weight[:, None, :]).astype(jnp.bfloat16)
    scaled_empty = (row_values * empty_weight[:, None, :]).astype(jnp.bfloat16)
    orbital_count = rows_full.shape[1]
    half_rows = scaled_full.shape[0] * scaled_full.shape[1]
    stacked = jnp.concatenate(
        (
            scaled_full.reshape(half_rows, orbital_count),
            scaled_empty.reshape(half_rows, orbital_count),
        ),
        axis=0,
    )
    col_count = column_orbitals.shape[0] * lax.axis_size("space")
    columns = lax.all_gather(column_orbitals, "tm", axis=1, tiled=True)
    greens = lax.dot_general(
        stacked,
        lax.all_gather(columns, "space", axis=0, tiled=True),
        (((1,), (1,)), ((), ())),
        preferred_element_type=jnp.float32,
    )
    product = (greens[:half_rows] * greens[half_rows:]).astype(jnp.bfloat16)
    time_count = times.shape[0]
    gathered = product.reshape(time_count, half_rows // time_count, col_count)
    sub_rows = gathered.shape[1]
    cosines = quad_weights[None, :] * jnp.cos(freqs[:, None] * times[None, :])
    spectrum = jnp.dot(
        cosines,
        gathered.reshape(time_count, sub_rows * col_count).astype(jnp.float32),
        precision=lax.Precision.HIGHEST,
    )
    return spectrum.reshape(freqs.shape[0], sub_rows, col_count)


def solution(mesh):
    placed = (P("space", "tm"), P("space", "tm"), P(), P(), P(), P(), P(), P())
    return jax.shard_map(
        body, mesh=mesh, in_specs=placed, out_specs=P(None, ("space", "tm"), None), check_vma=False
    )
```

profile of v0, /device:TPU:0, one launch (start us, length us, event | category | flops | bytes accessed | tf_op | source)
XLA Modules:
  0.0 66.5 jit_solution(772920246954484222)
XLA Ops:
  6.5 0.0 copy-start
  6.5 0.0 all-gather.2.cloned.1.call-start
  6.5 7.3 %all_gather.6 = bf16[16,2048]{1,0:T(8,128)(2,1)} all-gather(bf16[16,1024]{1,0:T(8,128)(2,1)} %param.9), channel_id=1, replica_groups=mesh['space'=16,'tm'=2] {'tm'}, dimensions={1}, use_global_device_ids=true | all-gather | bytes 98304 | tf_op jit(solution)/shard_map/all_gather | solution.py:27
  13.9 0.0 all-gather.2.cloned.1.call-update
  13.9 3.6 %all-to-all-start = ((bf16[2,256,1024]{2,1,0:T(8,128)(2,1)}), bf16[2,256,1024]{2,1,0:T(8,128)(2,1)S(1)}, u32[]{:S(2)}, u32[]{:S(2)}) async-start(bf16[2,256,1024]{2,1,0:T(8,128)(2,1)} %bitcast.18), calls=%async_computation | async-start | bytes 2097152 | tf_op jit(solution)/shard_map/all_to_all | solution.py:10
  17.5 0.0 copy-done.1
  17.5 0.0 copy-done
  17.5 0.0 copy-start.2
  17.5 0.0 copy-start.3
  17.5 11.8 %gather_fusion = f32[2048]{0:T(1024)S(1)} fusion(f32[2048]{0:T(1024)S(1)} %copy-done, s32[2048]{0:T(1024)S(1)} %fusion.7), kind=kCustom, calls=%fused_computation | custom fusion | bytes 24576 | tf_op jit(solution)/shard_map/jit(_take)/gather | solution.py:8
  29.3 0.0 copy-done.2
  29.4 0.0 copy-done.3
  29.4 0.1 fusion.6
  29.5 1.0 %all-to-all-done = bf16[2,256,1024]{2,1,0:T(8,128)(2,1)S(1)} async-done(((bf16[2,256,1024]{2,1,0:T(8,128)(2,1)}), bf16[2,256,1024]{2,1,0:T(8,128)(2,1)S(1)}, u32[]{:S(2)}, u32[]{:S(2)}) %all-to-all-start) | async-done | bytes 1048608 | tf_op jit(solution)/shard_map/all_to_all | solution.py:10
  30.5 0.2 convert_bitcast_fusion
  30.7 1.8 %copy.12 = f32[256,2,1024]{0,2,1:T(8,128)} copy(f32[256,2,1024]{2,0,1:T(8,128)S(1)} %convert_bitcast_fusion) | data formatting | bytes 4194304 | tf_op jit(solution)/shard_map/convert_element_type | solution.py:14
  32.5 1.9 %copy.13 = f32[256,2048]{1,0:T(8,128)S(1)} copy(f32[256,2048]{0,1:T(8,128)} %bitcast.14) | data formatting | bytes 4194304 | tf_op jit(solution)/shard_map/convert_element_type | solution.py:14
  34.4 3.1 %multiply_convert_fusion.1 = (bf16[2,256,2048]{2,1,0:T(8,128)(2,1)}, bf16[2,256,2048]{2,1,0:T(8,128)(2,1)}) fusion(f32[2,2048]{1,0:T(2,128)S(1)} %get-tuple-element.7, f32[256,2048]{1,0:T(8,128)S(1)} %copy.13, f32[2,2048]{1,0:T(2,128)S(1)} %get-tuple-element.8), kind=kLoop, calls=%fused_computation.6 | loop fusion | flops 4194304 | bytes 6324224 | tf_op jit(solution)/shard_map/convert_element_type | solution.py:15
  37.5 14.8 %all-gather.2.cloned.1.call-done = bf16[256,2048]{1,0:T(8,128)(2,1)} async-done(((bf16[16,2048]{1,0:T(8,128)(2,1)}), bf16[256,2048]{1,0:T(8,128)(2,1)}) %all-gather.2.cloned.1.call-update) | async-done | bytes 1048592 | tf_op jit(solution)/shard_map/all_gather | solution.py:30
  52.3 3.8 %fusion = f32[1024,256]{1,0:T(8,128)S(1)} fusion(bf16[256,2048]{1,0:T(8,128)(2,1)} %all-gather.2.cloned.1.call-done, bf16[512,2048]{1,0:T(8,128)(2,1)} %bitcast.16, bf16[512,2048]{1,0:T(8,128)(2,1)} %bitcast.15), kind=kOutput, calls=%fused_computation.1 | convolution fusion | flops 1082130432 | bytes 6291456 | tf_op jit(solution)/shard_map/dot_general | solution.py:28
  56.2 0.1 fusion.4
  56.2 0.1 reshape_reshape.3
  56.3 1.3 %fusion.8 = f32[8,256,256]{2,0,1:T(8,128)S(1)} fusion(bf16[256,256,2]{1,2,0:T(2,128)(2,1)S(1)} %bitcast.17, f32[8]{0:T(128)S(1)} %copy-done.4, f32[2]{0:T(128)S(1)} %copy-done.5, f32[2]{0:T(128)S(1)} %copy-done.3), kind=kOutput, calls=%fused_computation.18 | convolution fusion | flops 12582944 | bytes 2359344 | tf_op jit(solution)/shard_map/dot_general | solution.py:39
  57.7 2.0 %copy.14 = f32[8,256,256]{2,1,0:T(8,128)} copy(f32[8,256,256]{2,0,1:T(8,128)S(1)} %fusion.8) | data formatting | bytes 4194304 | tf_op jit(solution)/shard_map/dot_general | solution.py:39
  (8 shorter events, 0.0 us)
Async XLA Ops:
  6.5 11.0 %copy-start = (f32[2048]{0:T(1024)S(1)}, f32[2048]{0:T(1024)}, u32[]{:S(2)}) copy-start(f32[2048]{0:T(1024)} %param.12) | copy-start | bytes 24580
  6.5 10.9 %copy-start.1 = (s32[2048]{0:T(1024)S(1)}, s32[2048]{0:T(1024)}, u32[]{:S(2)}) copy-start(s32[2048]{0:T(1024)} %param.11) | copy-start | bytes 24580
  6.5 45.8 %all-gather.2.cloned.1.call-start = ((), (), s32[]{:S(2)}) async-start(), calls=%async_computation.1 | async-start | bytes 1114112 | tf_op jit(solution)/shard_map/all_gather | solution.py:30
  13.9 16.6 %all-to-all-start = ((bf16[2,256,1024]{2,1,0:T(8,128)(2,1)}), bf16[2,256,1024]{2,1,0:T(8,128)(2,1)S(1)}, u32[]{:S(2)}, u32[]{:S(2)}) async-start(bf16[2,256,1024]{2,1,0:T(8,128)(2,1)} %bitcast.18), calls=%async_computation | async-start | bytes 2097152 | tf_op jit(solution)/shard_map/all_to_all | solution.py:10
  17.5 11.8 %copy-start.2 = (s32[2048]{0:T(1024)S(1)}, s32[2048]{0:T(1024)}, u32[]{:S(2)}) copy-start(s32[2048]{0:T(1024)} %param.10) | copy-start | bytes 24580
  17.5 11.8 %copy-start.3 = (f32[2]{0:T(128)S(1)}, f32[2]{0:T(128)}, u32[]{:S(2)}) copy-start(f32[2]{0:T(128)} %param.13) | copy-start | bytes 28
  52.3 4.0 %copy-start.4 = (f32[8]{0:T(128)S(1)}, f32[8]{0:T(128)}, u32[]{:S(2)}) copy-start(f32[8]{0:T(128)} %param.15) | copy-start | bytes 100
  52.3 4.0 %copy-start.5 = (f32[2]{0:T(128)S(1)}, f32[2]{0:T(128)}, u32[]{:S(2)}) copy-start(f32[2]{0:T(128)} %param.14) | copy-start | bytes 28
Sparse Core Ops, SparseCore 0:
  14.0 38.2 all-gather.1
where the time goes:
time: 66.8 us; the launch traced here: 66.5 us
  local copies, waits for them, and re-layouts  17.6 us (26%)
  waiting for transfers between devices  15.8 us (24%)
  between operations  13.5 us (20%)
  blocking collectives  7.31 us (11%)
  matrix products  5.14 us (8%)
  starting transfers between devices  3.6 us (5%)
  other arithmetic  3.46 us (5%)
    all_gather x1, waiting for transfers between devices, body(): lax.all_gather(columns, 'space', axis=0, tiled=True)  14.8 us
    gather x1, local copies, waits for them, and re-layouts, body(): energy = jnp.take(levels, order)  11.8 us
    all_gather x1, blocking collectives, body(): columns = lax.all_gather(column_orbitals, 'tm', axis=1, tiled=True)  7.31 us
    dot_general x1, matrix products, body(): lax.dot_general(stacked, lax.all_gather(columns, 'space', axis=0, tiled=T...  3.8 us
    convert_element_type x2, local copies, waits for them, and re-layouts, body(): row_values = rows_full.astype(jnp.float32)[None]  3.73 us
    all_to_all x1, starting transfers between devices, body(): lax.all_to_all(row_orbitals, 'tm', split_axis=0, concat_axis=1, tiled=True)  3.59 us
    convert_element_type x1, other arithmetic, body(): scaled_full = (row_values * full_weight[:, None, :]).astype(jnp.bfloat16)  3.07 us
    dot_general x1, local copies, waits for them, and re-layouts, body(): jnp.dot(cosines, gathered.reshape(time_count, sub_rows * col_count).astyp...  1.96 us
  transfers between devices with their start and end apart: 2, of which 2 were waited for; matrix products, arithmetic and copies ran while one was open for 28% of the time, Pallas kernels for 0%

commit v1 on v0

--- a/solution.py
+++ b/solution.py
@@ -24,7 +24,7 @@
         axis=0,
     )
     col_count = column_orbitals.shape[0] * lax.axis_size("space")
-    columns = lax.all_gather(column_orbitals, "tm", axis=1, tiled=True)
+    columns = jnp.concatenate(lax.all_gather(column_orbitals, "tm"), axis=1)
     greens = lax.dot_general(
         stacked,
         lax.all_gather(columns, "space", axis=0, tiled=True),

time: 66.8 us -> 67.3 us (level)
  blocking collectives: 7.31 us -> 5.91 us
  waiting for transfers between devices: 15.8 us -> 17.1 us
  local copies, waits for them, and re-layouts: 17.6 us -> 18.3 us
    all_gather x1, blocking collectives: 7.31 us -> 5.91 us  [body(): columns = jnp.concatenate(lax.all_gather(column_orbitals, 'tm'), axis=1)]
    all_gather x1, waiting for transfers between devices: 14.8 us -> 16.1 us  [body(): lax.all_gather(columns, 'space', axis=0, tiled=True)]
where the time goes in v1:
time: 67.3 us; the launch traced here: 67.1 us
  local copies, waits for them, and re-layouts  18.3 us (27%)
  waiting for transfers between devices  17.1 us (25%)
  between operations  13.5 us (20%)
  blocking collectives  5.91 us (9%)
  matrix products  5.14 us (8%)
  starting transfers between devices  3.6 us (5%)
  other arithmetic  3.46 us (5%)
    all_gather x1, waiting for transfers between devices, body(): lax.all_gather(columns, 'space', axis=0, tiled=True)  16.1 us
    gather x1, local copies, waits for them, and re-layouts, body(): energy = jnp.take(levels, order)  11.8 us
    all_gather x1, blocking collectives, body(): columns = jnp.concatenate(lax.all_gather(column_orbitals, 'tm'), axis=1)  5.91 us
    dot_general x1, matrix products, body(): lax.dot_general(stacked, lax.all_gather(columns, 'space', axis=0, tiled=T...  3.8 us
    convert_element_type x2, local copies, waits for them, and re-layouts, body(): row_values = rows_full.astype(jnp.float32)[None]  3.73 us
    all_to_all x1, starting transfers between devices, body(): lax.all_to_all(row_orbitals, 'tm', split_axis=0, concat_axis=1, tiled=True)  3.59 us
    convert_element_type x1, other arithmetic, body(): scaled_full = (row_values * full_weight[:, None, :]).astype(jnp.bfloat16)  3.07 us
    dot_general x1, local copies, waits for them, and re-layouts, body(): jnp.dot(cosines, gathered.reshape(time_count, sub_rows * col_count).astyp...  1.96 us
  transfers between devices with their start and end apart: 2, of which 2 were waited for; matrix products, arithmetic and copies ran while one was open for 28% of the time, Pallas kernels for 0%

profile of v1, /device:TPU:0, one launch (start us, length us, event | category | flops | bytes accessed | tf_op | source)
XLA Modules:
  0.0 67.1 jit_solution(7302509247222079370)
XLA Ops:
  6.5 0.0 copy-start
  6.5 0.0 all-gather.3.cloned.1.call-start
  6.5 5.9 %all-gather = bf16[32,1024]{1,0:T(8,128)(2,1)S(1)} all-gather(bf16[16,1024]{1,0:T(8,128)(2,1)} %param.9), channel_id=2, replica_groups=mesh['space'=16,'tm'=2] {'tm'}, dimensions={0}, use_global_device_ids=true | all-gather | bytes 98304 | tf_op jit(solution)/shard_map/all_gather | solution.py:27
  12.5 0.1 copy.15
  12.5 0.6 copy.17
  13.2 0.0 all-gather.3.cloned.1.call-update
  13.2 3.6 %all-to-all-start = ((bf16[2,256,1024]{2,1,0:T(8,128)(2,1)}), bf16[2,256,1024]{2,1,0:T(8,128)(2,1)S(1)}, u32[]{:S(2)}, u32[]{:S(2)}) async-start(bf16[2,256,1024]{2,1,0:T(8,128)(2,1)} %bitcast.22), calls=%async_computation | async-start | bytes 2097152 | tf_op jit(solution)/shard_map/all_to_all | solution.py:10
  16.8 0.0 copy-start.2
  16.8 0.0 copy-start.3
  16.8 11.8 %gather_fusion = f32[2048]{0:T(1024)S(1)} fusion(f32[2048]{0:T(1024)S(1)} %copy-done, s32[2048]{0:T(1024)S(1)} %fusion.7), kind=kCustom, calls=%fused_computation | custom fusion | bytes 24576 | tf_op jit(solution)/shard_map/jit(_take)/gather | solution.py:8
  28.7 0.1 fusion.6
  28.8 1.0 %all-to-all-done = bf16[2,256,1024]{2,1,0:T(8,128)(2,1)S(1)} async-done(((bf16[2,256,1024]{2,1,0:T(8,128)(2,1)}), bf16[2,256,1024]{2,1,0:T(8,128)(2,1)S(1)}, u32[]{:S(2)}, u32[]{:S(2)}) %all-to-all-start) | async-done | bytes 1048608 | tf_op jit(solution)/shard_map/all_to_all | solution.py:10
  29.8 0.2 convert_bitcast_fusion
  30.0 1.8 %copy.13 = f32[256,2,1024]{0,2,1:T(8,128)} copy(f32[256,2,1024]{2,0,1:T(8,128)S(1)} %convert_bitcast_fusion) | data formatting | bytes 4194304 | tf_op jit(solution)/shard_map/convert_element_type | solution.py:14
  31.8 1.9 %copy.14 = f32[256,2048]{1,0:T(8,128)S(1)} copy(f32[256,2048]{0,1:T(8,128)} %bitcast.18) | data formatting | bytes 4194304 | tf_op jit(solution)/shard_map/convert_element_type | solution.py:14
  33.8 3.1 %multiply_convert_fusion.1 = (bf16[2,256,2048]{2,1,0:T(8,128)(2,1)}, bf16[2,256,2048]{2,1,0:T(8,128)(2,1)}) fusion(f32[2,2048]{1,0:T(2,128)S(1)} %get-tuple-element.7, f32[256,2048]{1,0:T(8,128)S(1)} %copy.14, f32[2,2048]{1,0:T(2,128)S(1)} %get-tuple-element.8), kind=kLoop, calls=%fused_computation.6 | loop fusion | flops 4194304 | bytes 6324224 | tf_op jit(solution)/shard_map/convert_element_type | solution.py:15
  36.8 16.1 %all-gather.3.cloned.1.call-done = bf16[256,2048]{1,0:T(8,128)(2,1)} async-done(((bf16[16,2048]{1,0:T(8,128)(2,1)}), bf16[256,2048]{1,0:T(8,128)(2,1)}) %all-gather.3.cloned.1.call-update) | async-done | bytes 1048592 | tf_op jit(solution)/shard_map/all_gather | solution.py:30
  52.9 3.8 %fusion = f32[1024,256]{1,0:T(8,128)S(1)} fusion(bf16[256,2048]{1,0:T(8,128)(2,1)} %all-gather.3.cloned.1.call-done, bf16[512,2048]{1,0:T(8,128)(2,1)} %bitcast.20, bf16[512,2048]{1,0:T(8,128)(2,1)} %bitcast.19), kind=kOutput, calls=%fused_computation.1 | convolution fusion | flops 1082130432 | bytes 6291456 | tf_op jit(solution)/shard_map/dot_general | solution.py:28
  56.8 0.1 fusion.4
  56.8 0.1 reshape_reshape.3
  56.9 0.0 copy-done.4
  56.9 0.0 copy-done.5
  56.9 1.3 %fusion.8 = f32[8,256,256]{2,0,1:T(8,128)S(1)} fusion(bf16[256,256,2]{1,2,0:T(2,128)(2,1)S(1)} %bitcast.21, f32[8]{0:T(128)S(1)} %copy-done.4, f32[2]{0:T(128)S(1)} %copy-done.5, f32[2]{0:T(128)S(1)} %copy-done.3), kind=kOutput, calls=%fused_computation.18 | convolution fusion | flops 12582944 | bytes 2359344 | tf_op jit(solution)/shard_map/dot_general | solution.py:39
  58.3 2.0 %copy.16 = f32[8,256,256]{2,1,0:T(8,128)} copy(f32[8,256,256]{2,0,1:T(8,128)S(1)} %fusion.8) | data formatting | bytes 4194304 | tf_op jit(solution)/shard_map/dot_general | solution.py:39
  (10 shorter events, 0.0 us)
Async XLA Ops:
  6.5 10.3 %copy-start = (f32[2048]{0:T(1024)S(1)}, f32[2048]{0:T(1024)}, u32[]{:S(2)}) copy-start(f32[2048]{0:T(1024)} %param.12) | copy-start | bytes 24580
  6.5 10.2 %copy-start.1 = (s32[2048]{0:T(1024)S(1)}, s32[2048]{0:T(1024)}, u32[]{:S(2)}) copy-start(s32[2048]{0:T(1024)} %param.11) | copy-start | bytes 24580
  6.5 46.4 %all-gather.3.cloned.1.call-start = ((), (), s32[]{:S(2)}) async-start(), calls=%async_computation.1 | async-start | bytes 1114112 | tf_op jit(solution)/shard_map/all_gather | solution.py:30
  13.2 16.6 %all-to-all-start = ((bf16[2,256,1024]{2,1,0:T(8,128)(2,1)}), bf16[2,256,1024]{2,1,0:T(8,128)(2,1)S(1)}, u32[]{:S(2)}, u32[]{:S(2)}) async-start(bf16[2,256,1024]{2,1,0:T(8,128)(2,1)} %bitcast.22), calls=%async_computation | async-start | bytes 2097152 | tf_op jit(solution)/shard_map/all_to_all | solution.py:10
  16.8 11.8 %copy-start.2 = (s32[2048]{0:T(1024)S(1)}, s32[2048]{0:T(1024)}, u32[]{:S(2)}) copy-start(s32[2048]{0:T(1024)} %param.10) | copy-start | bytes 24580
  16.8 11.8 %copy-start.3 = (f32[2]{0:T(128)S(1)}, f32[2]{0:T(128)}, u32[]{:S(2)}) copy-start(f32[2]{0:T(128)} %param.13) | copy-start | bytes 28
  52.9 3.9 %copy-start.4 = (f32[8]{0:T(128)S(1)}, f32[8]{0:T(128)}, u32[]{:S(2)}) copy-start(f32[8]{0:T(128)} %param.15) | copy-start | bytes 100
  52.9 4.0 %copy-start.5 = (f32[2]{0:T(128)S(1)}, f32[2]{0:T(128)}, u32[]{:S(2)}) copy-start(f32[2]{0:T(128)} %param.14) | copy-start | bytes 28
Sparse Core Ops, SparseCore 0:
  13.3 39.5 all-gather.2
